TPU v7x, 512 devices: a whole 4x8x8 slice. The times are simulated.
512 devices in a mesh: sub: 64 (over y, x, core), crs: 8 (over z).
Axes of the slice: x: 4, y: 8, z: 8, core: 2. Of those that a mesh axis runs over, the one named last changes fastest.
Arguments:
- multipliers: float32 [16, 2048, 512], P(None, ('sub', 'crs')), may hold values from -6 to 6
- own_modes: float32 [6, 2048, 512], P(None, ('sub', 'crs')), may hold values from -0.75 to 0.75
- neighbour_modes: float32 [6, 2048, 512], P(None, ('sub', 'crs')), may hold values from -0.75 to 0.75
- face_index: int32 [2048, 512], P(('sub', 'crs')), may hold values from 0 to 5, as said below
- neighbour_list: int32 [2048, 6], replicated, may hold values from 0 to 2047, as said below
- coarse_factor: float32 [12288, 12288], P('sub', 'crs'), may hold values from -0.0546875 to 0.0546875
Outputs:
- projected: float32 [16, 2048, 512], P(None, ('sub', 'crs'))
Inputs may be any that keep to these rules, and one draw needn't show every extreme that they name: `face_index`: the multipliers of each subdomain lie in 6 contiguous nonempty blocks, face 0 first and face 5 last. `neighbour_list`: subdomain s = (32 x + y) * 32 + z sits at (x, y, z) of a periodic grid of 2 x 32 x 32 subdomains; the 6 faces of each subdomain name its grid neighbours x plus 1, x minus 1, y plus or minus 1, z plus or minus 1 (periodic; along the first dimension both name the same subdomain), in an order that differs from subdomain to subdomain.
All inputs are finite; a program needn't handle non-finite values.
Results may differ from a plain program's by a relative error of at most 0.0001.
Values sent between devices are 32-bit elements; how exact they have to be, the bound alone decides.
A program may use at most 64 MiB of HBM per device.

v0:
```python
import jax
import jax.numpy as jnp
from jax import lax
from jax.sharding import PartitionSpec as P

MODES = 6
NFACE = 6


HIGHEST = lax.Precision.HIGHEST


def shifted(value, axis, by):
    peers = lax.axis_size(axis)
    return lax.ppermute(value, axis, [(i, (i + by) % peers) for i in range(peers)])


def copy_for_each(value, axis):
    copies = jnp.broadcast_to(value, (lax.axis_size(axis), *value.shape))
    return lax.all_to_all(copies, axis, split_axis=0, concat_axis=0, tiled=True)


def laid_out(parts, dim):
    lengths = list(parts.shape[1:])
    lengths[dim] *= parts.shape[0]
    return jnp.moveaxis(parts, 0, dim).reshape(lengths)


def gathered_copies(value, axis, dim):
    parts = copy_for_each(value, axis)
    return laid_out(parts, dim)


def in_blocks(value, dim, peers):
    before, after = (value.shape[:dim], value.shape[dim + 1 :])
    return jnp.moveaxis(value.reshape(*before, peers, -1, *after), dim, 0)


def sent_and_summed(value, axis, dim):
    parts = in_blocks(value, dim, lax.axis_size(axis))
    arrived = lax.all_to_all(parts, axis, split_axis=0, concat_axis=0, tiled=True)
    return arrived.sum(axis=0)


def padded_to(lines, peers):
    spare = -lines.shape[0] % peers
    if not spare:
        return lines
    return jnp.concatenate([lines, jnp.zeros((spare, *lines.shape[1:]), lines.dtype)])


def nested_sum(value, axes):
    lines = value.reshape(-1, value.shape[-1])
    own = sent_and_summed(padded_to(lines, lax.axis_size(axes)), axes, 0)
    whole = gathered_copies(own, axes, 0)
    return whole[: len(lines)].reshape(value.shape)


def body(multipliers, own_modes, neighbour_modes, face_index, neighbour_list, coarse_factor):
    width_rhs = multipliers.shape[0]
    local_subs = multipliers.shape[1]
    crs_size = lax.axis_size("crs")
    sub_size = lax.axis_size("sub")
    crs_rank = lax.axis_index("crs")
    sub_rank = lax.axis_index("sub")
    group_subs = local_subs * crs_size
    first_sub = (sub_rank * crs_size + crs_rank) * local_subs
    row_len = sub_size // 2
    col_len = sub_size // row_len
    row_place = sub_rank % row_len
    local_ids = first_sub + lax.iota(jnp.int32, local_subs)
    first = local_ids // (row_len * group_subs)
    second = local_ids // group_subs % row_len
    third = local_ids % group_subs

    def place(a, b, c):
        return (a * row_len + b) * group_subs + c

    grid_next = jnp.stack(
        [
            place((first + 1) % col_len, second, third),
            place((first + col_len - 1) % col_len, second, third),
            place(first, (second + 1) % row_len, third),
            place(first, (second + row_len - 1) % row_len, third),
            place(first, second, (third + 1) % group_subs),
            place(first, second, (third + group_subs - 1) % group_subs),
        ],
        axis=1,
    )
    local_nbrs = lax.dynamic_slice_in_dim(neighbour_list, first_sub, local_subs, 0)
    matches = (local_nbrs[:, :, None] == grid_next[:, None, :]).astype(jnp.int32)
    first_hit = matches * (jnp.cumsum(matches, axis=2) == 1).astype(jnp.int32)
    face_dir = first_hit.astype(jnp.float32)
    masked_modes = []
    for which_face in range(NFACE):
        masked_modes.append(neighbour_modes * (face_index == which_face).astype(jnp.float32)[None])
    own_coarse = jnp.einsum("ksm,rsm->krs", own_modes, multipliers, precision=HIGHEST)
    face_parts = []
    for which_face in range(NFACE):
        face_parts.append(
            jnp.einsum("ksm,rsm->krs", masked_modes[which_face], multipliers, precision=HIGHEST)
        )
    face_stack = jnp.stack(face_parts, axis=3)
    outgoing = jnp.einsum("krjf,jfd->dkrj", face_stack, face_dir, precision=HIGHEST)
    plans = [(0, row_len), (1, -row_len), (2, 1), (2, 1 - row_len), (3, -1), (3, row_len - 1)]
    arrived = []
    for direction, step in plans:
        arrived.append(shifted(outgoing[direction], "sub", step))
    plus_y = jnp.where(row_place == 0, arrived[3], arrived[2])
    minus_y = jnp.where(row_place == row_len - 1, arrived[5], arrived[4])
    upward = outgoing[4]
    downward = outgoing[5]
    crossing = []
    for piece, step in ((upward[:, :, -1:], 1), (downward[:, :, :1], -1)):
        crossing.append(shifted(piece, "crs", step))
    from_below = jnp.concatenate([crossing[0], upward[:, :, :-1]], axis=2)
    from_above = jnp.concatenate([downward[:, :, 1:], crossing[1]], axis=2)
    own_total = own_coarse + arrived[0] + arrived[1] + plus_y + minus_y + from_below + from_above
    group_coarse = gathered_copies(own_total, "crs", 2)
    coarse_rhs = group_coarse.transpose(2, 0, 1).reshape(group_subs * MODES, width_rhs)
    partial_rows = jnp.einsum("cp,cr->pr", coarse_factor, coarse_rhs, precision=HIGHEST)
    panel_rows = nested_sum(partial_rows, "sub")
    partial_modes = jnp.dot(
        coarse_factor, panel_rows, precision=HIGHEST, preferred_element_type=jnp.float32
    )
    partial_modes = partial_modes.reshape(group_subs, MODES, width_rhs).transpose(1, 2, 0)
    own_amps = sent_and_summed(partial_modes, "crs", 2)
    fetched = []
    for step in (-row_len, row_len, -1, row_len - 1, 1, 1 - row_len):
        fetched.append(shifted(own_amps, "sub", step))
    plus_y = jnp.where(row_place == row_len - 1, fetched[3], fetched[2])
    minus_y = jnp.where(row_place == 0, fetched[5], fetched[4])
    edges = []
    for piece, step in ((own_amps[:, :, :1], -1), (own_amps[:, :, -1:], 1)):
        edges.append(shifted(piece, "crs", step))
    plus_z = jnp.concatenate([own_amps[:, :, 1:], edges[0]], axis=2)
    minus_z = jnp.concatenate([edges[1], own_amps[:, :, :-1]], axis=2)
    stacked = jnp.stack([fetched[0], fetched[1], plus_y, minus_y, plus_z, minus_z])
    near_amps = jnp.einsum("dkrj,jfd->krjf", stacked, face_dir, precision=HIGHEST)
    applied = jnp.einsum("ksm,krs->rsm", own_modes, own_amps, precision=HIGHEST)
    for which_face in range(NFACE):
        applied = applied + jnp.einsum(
            "ksm,krs->rsm",
            masked_modes[which_face],
            near_amps[:, :, :, which_face],
            precision=HIGHEST,
        )
    return multipliers - applied


def solution(mesh):
    placed = (
        P(None, ("sub", "crs"), None),
        P(None, ("sub", "crs"), None),
        P(None, ("sub", "crs"), None),
        P(("sub", "crs"), None),
        P(),
        P("sub", "crs"),
    )
    return jax.shard_map(
        body, mesh=mesh, in_specs=placed, out_specs=P(None, ("sub", "crs"), None), check_vma=False
    )
```

profile of v0, /device:TPU:1, one launch (start us, length us, event | category | flops | bytes accessed | tf_op | source)
XLA Modules:
  0.0 147.0 jit_solution(17944421383802147151)
XLA Ops:
  0.1 0.9 constant_dynamic-slice_fusion
  1.2 0.6 reduce_window_sum.11
  1.8 0.7 compare_convert_fusion.1
  2.6 0.8 broadcast_multiply_fusion
  3.5 1.2 fusion.7
  4.7 1.2 fusion.6
  7.1 0.4 fusion.15
  7.5 8.3 %collective-permute-start.1 = (f32[6,16,4]{1,0,2:T(8,128)S(1)}, f32[6,16,4]{1,0,2:T(8,128)S(1)}, u32[]{:S(2)}, u32[]{:S(2)}) collective-permute-start(f32[6,16,4]{1,0,2:T(8,128)S(1)} %get-tuple-element.15), channel_id=1, source_target_pairs={{0,256},{8,264},{16,272},{24,280},{32,288},{40,296},{48,304},{56,3... | collective-permute-start | bytes 4616 | tf_op jit(solution)/shard_map/ppermute | solution.py:15
  15.8 4.0 %collective-permute-start.6 = (f32[6,16,1]{1,0,2:T(8,128)S(1)}, f32[6,16,1]{1,0,2:T(8,128)S(1)}, u32[]{:S(2)}, u32[]{:S(2)}) collective-permute-start(f32[6,16,1]{1,0,2:T(8,128)S(1)} %slice.87), channel_id=1, source_target_pairs={{0,1},{1,2},{2,3},{3,4},{4,5},{5,6},{6,7},{7,0},{8,9},{9,10},{10,1... | collective-permute-start | bytes 1160 | tf_op jit(solution)/shard_map/ppermute | solution.py:15
  19.8 8.6 %collective-permute-start.7 = (f32[6,16,1]{1,0,2:T(8,128)S(1)}, f32[6,16,1]{1,0,2:T(8,128)S(1)}, u32[]{:S(2)}, u32[]{:S(2)}) collective-permute-start(f32[6,16,1]{1,0,2:T(8,128)S(1)} %slice.91), channel_id=1, source_target_pairs={{0,7},{1,0},{2,1},{3,2},{4,3},{5,4},{6,5},{7,6},{8,15},{9,8},{10,9... | collective-permute-start | bytes 1160 | tf_op jit(solution)/shard_map/ppermute | solution.py:15
  28.4 4.2 %collective-permute-start.3 = (f32[6,16,4]{1,0,2:T(8,128)S(1)}, f32[6,16,4]{1,0,2:T(8,128)S(1)}, u32[]{:S(2)}, u32[]{:S(2)}) collective-permute-start(f32[6,16,4]{1,0,2:T(8,128)S(1)} %get-tuple-element.11), channel_id=1, source_target_pairs={{0,8},{8,16},{16,24},{24,32},{32,40},{40,48},{48,56},{56,64},{64,7... | collective-permute-start | bytes 4616 | tf_op jit(solution)/shard_map/ppermute | solution.py:15
  32.7 1.9 %collective-permute-start.2 = (f32[6,16,4]{1,0,2:T(8,128)S(1)}, f32[6,16,4]{1,0,2:T(8,128)S(1)}, u32[]{:S(2)}, u32[]{:S(2)}) collective-permute-start(f32[6,16,4]{1,0,2:T(8,128)S(1)} %get-tuple-element.11), channel_id=1, source_target_pairs={{0,264},{8,272},{16,280},{24,288},{32,296},{40,304},{48,312},{56,3... | collective-permute-start | bytes 4616 | tf_op jit(solution)/shard_map/ppermute | solution.py:15
  34.6 7.0 %collective-permute-start = (f32[6,16,4]{1,0,2:T(8,128)S(1)}, f32[6,16,4]{1,0,2:T(8,128)S(1)}, u32[]{:S(2)}, u32[]{:S(2)}) collective-permute-start(f32[6,16,4]{1,0,2:T(8,128)S(1)} %get-tuple-element.16), channel_id=1, source_target_pairs={{0,256},{8,264},{16,272},{24,280},{32,288},{40,296},{48,304},{56,3... | collective-permute-start | bytes 4616 | tf_op jit(solution)/shard_map/ppermute | solution.py:15
  41.6 2.9 %collective-permute-start.5 = (f32[6,16,4]{1,0,2:T(8,128)S(1)}, f32[6,16,4]{1,0,2:T(8,128)S(1)}, u32[]{:S(2)}, u32[]{:S(2)}) collective-permute-start(f32[6,16,4]{1,0,2:T(8,128)S(1)} %get-tuple-element.14), channel_id=1, source_target_pairs={{0,504},{8,0},{16,8},{24,16},{32,24},{40,32},{48,40},{56,48},{64,5... | collective-permute-start | bytes 4616 | tf_op jit(solution)/shard_map/ppermute | solution.py:15
  44.5 5.1 %collective-permute-start.4 = (f32[6,16,4]{1,0,2:T(8,128)S(1)}, f32[6,16,4]{1,0,2:T(8,128)S(1)}, u32[]{:S(2)}, u32[]{:S(2)}) collective-permute-start(f32[6,16,4]{1,0,2:T(8,128)S(1)} %get-tuple-element.14), channel_id=1, source_target_pairs={{0,248},{8,256},{16,264},{24,272},{32,280},{40,288},{48,296},{56,3... | collective-permute-start | bytes 4616 | tf_op jit(solution)/shard_map/ppermute | solution.py:15
  49.7 4.7 %collective-permute-done.4 = f32[6,16,4]{1,0,2:T(8,128)S(1)} collective-permute-done((f32[6,16,4]{1,0,2:T(8,128)S(1)}, f32[6,16,4]{1,0,2:T(8,128)S(1)}, u32[]{:S(2)}, u32[]{:S(2)}) %collective-permute-start.4) | collective-permute-done | bytes 1568 | tf_op jit(solution)/shard_map/ppermute | solution.py:15
  54.8 10.6 %all_to_all.20 = f32[8,1,384]{2,1,0:T(1,128)S(1)} all-to-all(f32[8,1,384]{2,1,0:T(1,128)S(1)} %reshape.414), channel_id=1, replica_groups=mesh['sub'=64,'crs'=8] {'crs'}, dimensions={0} | all-to-all | bytes 24576 | tf_op jit(solution)/shard_map/all_to_all | solution.py:20
  65.4 0.5 broadcast.979
  65.9 0.7 reduce
  66.9 0.7 convolution_bitcast_fusion
  67.6 0.4 reshape.408
  68.3 0.4 reshape.416
  68.7 16.7 %all_to_all.21 = f32[64,1,384]{2,1,0:T(1,128)S(1)} all-to-all(f32[64,1,384]{2,1,0:T(1,128)S(1)} %reshape.416), channel_id=1, replica_groups=mesh['sub'=64,'crs'=8] {'sub'}, dimensions={0} | all-to-all | bytes 196608 | tf_op jit(solution)/shard_map/all_to_all | solution.py:41
  85.3 0.9 reduce.1
  86.2 0.3 reshape.417
  86.7 0.4 reshape.418
  87.1 14.3 %all_to_all.22 = f32[64,1,384]{2,1,0:T(1,128)S(1)} all-to-all(f32[64,1,384]{2,1,0:T(1,128)S(1)} %reshape.418), channel_id=1, replica_groups=mesh['sub'=64,'crs'=8] {'sub'}, dimensions={0} | all-to-all | bytes 196608 | tf_op jit(solution)/shard_map/all_to_all | solution.py:20
  101.4 0.9 reduce.2
  102.3 0.3 reshape.419
  103.1 1.0 convolution_bitcast_fusion.2
  104.4 9.0 %all_to_all.23 = f32[8,1,384]{2,1,0:T(1,128)S(1)} all-to-all(f32[8,1,384]{2,1,0:T(1,128)S(1)} %reshape.420), channel_id=1, replica_groups=mesh['sub'=64,'crs'=8] {'crs'}, dimensions={0} | all-to-all | bytes 24576 | tf_op jit(solution)/shard_map/all_to_all | solution.py:41
  113.4 0.7 reduce.3
  114.2 2.3 %collective-permute-start.8 = (f32[6,16,4]{1,0,2:T(8,128)S(1)}, f32[6,16,4]{1,0,2:T(8,128)S(1)}, u32[]{:S(2)}, u32[]{:S(2)}) collective-permute-start(f32[6,16,4]{1,0,2:T(8,128)S(1)} %copy.200), channel_id=1, source_target_pairs={{0,256},{8,264},{16,272},{24,280},{32,288},{40,296},{48,304},{56,3... | collective-permute-start | bytes 4616 | tf_op jit(solution)/shard_map/ppermute | solution.py:15
  116.5 0.4 fusion.36
  116.9 4.2 %collective-permute-start.12 = (f32[6,16,4]{1,0,2:T(8,128)S(1)}, f32[6,16,4]{1,0,2:T(8,128)S(1)}, u32[]{:S(2)}, u32[]{:S(2)}) collective-permute-start(f32[6,16,4]{1,0,2:T(8,128)S(1)} %copy.200), channel_id=1, source_target_pairs={{0,8},{8,16},{16,24},{24,32},{32,40},{40,48},{48,56},{56,64},{64,7... | collective-permute-start | bytes 4616 | tf_op jit(solution)/shard_map/ppermute | solution.py:15
  121.1 6.1 %collective-permute-start.11 = (f32[6,16,4]{1,0,2:T(8,128)S(1)}, f32[6,16,4]{1,0,2:T(8,128)S(1)}, u32[]{:S(2)}, u32[]{:S(2)}) collective-permute-start(f32[6,16,4]{1,0,2:T(8,128)S(1)} %copy.200), channel_id=1, source_target_pairs={{0,264},{8,272},{16,280},{24,288},{32,296},{40,304},{48,312},{56,3... | collective-permute-start | bytes 4616 | tf_op jit(solution)/shard_map/ppermute | solution.py:15
  127.2 2.6 %collective-permute-start.10 = (f32[6,16,4]{1,0,2:T(8,128)S(1)}, f32[6,16,4]{1,0,2:T(8,128)S(1)}, u32[]{:S(2)}, u32[]{:S(2)}) collective-permute-start(f32[6,16,4]{1,0,2:T(8,128)S(1)} %copy.200), channel_id=1, source_target_pairs={{0,504},{8,0},{16,8},{24,16},{32,24},{40,32},{48,40},{56,48},{64,5... | collective-permute-start | bytes 4616 | tf_op jit(solution)/shard_map/ppermute | solution.py:15
  129.8 6.5 %collective-permute-start.9 = (f32[6,16,4]{1,0,2:T(8,128)S(1)}, f32[6,16,4]{1,0,2:T(8,128)S(1)}, u32[]{:S(2)}, u32[]{:S(2)}) collective-permute-start(f32[6,16,4]{1,0,2:T(8,128)S(1)} %copy.200), channel_id=1, source_target_pairs={{0,248},{8,256},{16,264},{24,272},{32,280},{40,288},{48,296},{56,3... | collective-permute-start | bytes 4616 | tf_op jit(solution)/shard_map/ppermute | solution.py:15
  136.3 2.2 %collective-permute-start.14 = (f32[6,16,1]{1,0,2:T(8,128)S(1)}, f32[6,16,1]{1,0,2:T(8,128)S(1)}, u32[]{:S(2)}, u32[]{:S(2)}) collective-permute-start(f32[6,16,1]{1,0,2:T(8,128)S(1)} %get-tuple-element.23), channel_id=1, source_target_pairs={{0,1},{1,2},{2,3},{3,4},{4,5},{5,6},{6,7},{7,0},{8,9},{9,10},{10,1... | collective-permute-start | bytes 1160 | tf_op jit(solution)/shard_map/ppermute | solution.py:15
  138.6 4.3 %collective-permute-start.13 = (f32[6,16,1]{1,0,2:T(8,128)S(1)}, f32[6,16,1]{1,0,2:T(8,128)S(1)}, u32[]{:S(2)}, u32[]{:S(2)}) collective-permute-start(f32[6,16,1]{1,0,2:T(8,128)S(1)} %get-tuple-element.24), channel_id=1, source_target_pairs={{0,7},{1,0},{2,1},{3,2},{4,3},{5,4},{6,5},{7,6},{8,15},{9,8},{10,9... | collective-permute-start | bytes 1160 | tf_op jit(solution)/shard_map/ppermute | solution.py:15
  142.9 0.7 collective-permute-done.13
  144.1 0.4 convolution_add_fusion.5
  144.4 0.4 convolution_add_fusion.4
  144.8 0.4 convolution_add_fusion.3
  145.2 0.4 convolution_add_fusion.2
  145.5 0.4 convolution_add_fusion.1
  145.9 0.4 fusion.1
  146.2 0.7 copy.231
  (78 shorter events, 4.0 us)
Async XLA Ops:
  0.0 66.9 %copy-start = (f32[192,1536]{1,0:T(8,128)S(1)}, f32[192,1536]{1,0:T(8,128)}, u32[]{:S(2)}) copy-start(f32[192,1536]{1,0:T(8,128)} %param.11) | copy-start | bytes 3538948
  0.0 5.9 %copy-start.1 = (f32[16,4,512]{2,1,0:T(4,128)S(1)}, f32[16,4,512]{2,1,0:T(4,128)}, u32[]{:S(2)}) copy-start(f32[16,4,512]{2,1,0:T(4,128)} %param.6) | copy-start | bytes 393220
  2.6 51.8 %copy-start.2 = (f32[6,4,512]{2,1,0:T(4,128)S(1)}, f32[6,4,512]{2,1,0:T(4,128)}, u32[]{:S(2)}) copy-start(f32[6,4,512]{2,1,0:T(4,128)} %param.7) | copy-start | bytes 147460
  7.5 37.0 %collective-permute-start.1 = (f32[6,16,4]{1,0,2:T(8,128)S(1)}, f32[6,16,4]{1,0,2:T(8,128)S(1)}, u32[]{:S(2)}, u32[]{:S(2)}) collective-permute-start(f32[6,16,4]{1,0,2:T(8,128)S(1)} %get-tuple-element.15), channel_id=1, source_target_pairs={{0,256},{8,264},{16,272},{24,280},{32,288},{40,296},{48,304},{56,3... | collective-permute-start | bytes 4616 | tf_op jit(solution)/shard_map/ppermute | solution.py:15
  15.8 18.8 %collective-permute-start.6 = (f32[6,16,1]{1,0,2:T(8,128)S(1)}, f32[6,16,1]{1,0,2:T(8,128)S(1)}, u32[]{:S(2)}, u32[]{:S(2)}) collective-permute-start(f32[6,16,1]{1,0,2:T(8,128)S(1)} %slice.87), channel_id=1, source_target_pairs={{0,1},{1,2},{2,3},{3,4},{4,5},{5,6},{6,7},{7,0},{8,9},{9,10},{10,1... | collective-permute-start | bytes 1160 | tf_op jit(solution)/shard_map/ppermute | solution.py:15
  19.8 21.8 %collective-permute-start.7 = (f32[6,16,1]{1,0,2:T(8,128)S(1)}, f32[6,16,1]{1,0,2:T(8,128)S(1)}, u32[]{:S(2)}, u32[]{:S(2)}) collective-permute-start(f32[6,16,1]{1,0,2:T(8,128)S(1)} %slice.91), channel_id=1, source_target_pairs={{0,7},{1,0},{2,1},{3,2},{4,3},{5,4},{6,5},{7,6},{8,15},{9,8},{10,9... | collective-permute-start | bytes 1160 | tf_op jit(solution)/shard_map/ppermute | solution.py:15
  28.4 21.2 %collective-permute-start.3 = (f32[6,16,4]{1,0,2:T(8,128)S(1)}, f32[6,16,4]{1,0,2:T(8,128)S(1)}, u32[]{:S(2)}, u32[]{:S(2)}) collective-permute-start(f32[6,16,4]{1,0,2:T(8,128)S(1)} %get-tuple-element.11), channel_id=1, source_target_pairs={{0,8},{8,16},{16,24},{24,32},{32,40},{40,48},{48,56},{56,64},{64,7... | collective-permute-start | bytes 4616 | tf_op jit(solution)/shard_map/ppermute | solution.py:15
  32.7 17.0 %collective-permute-start.2 = (f32[6,16,4]{1,0,2:T(8,128)S(1)}, f32[6,16,4]{1,0,2:T(8,128)S(1)}, u32[]{:S(2)}, u32[]{:S(2)}) collective-permute-start(f32[6,16,4]{1,0,2:T(8,128)S(1)} %get-tuple-element.11), channel_id=1, source_target_pairs={{0,264},{8,272},{16,280},{24,288},{32,296},{40,304},{48,312},{56,3... | collective-permute-start | bytes 4616 | tf_op jit(solution)/shard_map/ppermute | solution.py:15
  34.6 15.0 %collective-permute-start = (f32[6,16,4]{1,0,2:T(8,128)S(1)}, f32[6,16,4]{1,0,2:T(8,128)S(1)}, u32[]{:S(2)}, u32[]{:S(2)}) collective-permute-start(f32[6,16,4]{1,0,2:T(8,128)S(1)} %get-tuple-element.16), channel_id=1, source_target_pairs={{0,256},{8,264},{16,272},{24,280},{32,288},{40,296},{48,304},{56,3... | collective-permute-start | bytes 4616 | tf_op jit(solution)/shard_map/ppermute | solution.py:15
  41.6 8.1 %collective-permute-start.5 = (f32[6,16,4]{1,0,2:T(8,128)S(1)}, f32[6,16,4]{1,0,2:T(8,128)S(1)}, u32[]{:S(2)}, u32[]{:S(2)}) collective-permute-start(f32[6,16,4]{1,0,2:T(8,128)S(1)} %get-tuple-element.14), channel_id=1, source_target_pairs={{0,504},{8,0},{16,8},{24,16},{32,24},{40,32},{48,40},{56,48},{64,5... | collective-permute-start | bytes 4616 | tf_op jit(solution)/shard_map/ppermute | solution.py:15
  44.5 9.9 %collective-permute-start.4 = (f32[6,16,4]{1,0,2:T(8,128)S(1)}, f32[6,16,4]{1,0,2:T(8,128)S(1)}, u32[]{:S(2)}, u32[]{:S(2)}) collective-permute-start(f32[6,16,4]{1,0,2:T(8,128)S(1)} %get-tuple-element.14), channel_id=1, source_target_pairs={{0,248},{8,256},{16,264},{24,272},{32,280},{40,288},{48,296},{56,3... | collective-permute-start | bytes 4616 | tf_op jit(solution)/shard_map/ppermute | solution.py:15
  114.2 22.1 %collective-permute-start.8 = (f32[6,16,4]{1,0,2:T(8,128)S(1)}, f32[6,16,4]{1,0,2:T(8,128)S(1)}, u32[]{:S(2)}, u32[]{:S(2)}) collective-permute-start(f32[6,16,4]{1,0,2:T(8,128)S(1)} %copy.200), channel_id=1, source_target_pairs={{0,256},{8,264},{16,272},{24,280},{32,288},{40,296},{48,304},{56,3... | collective-permute-start | bytes 4616 | tf_op jit(solution)/shard_map/ppermute | solution.py:15
  116.9 26.0 %collective-permute-start.12 = (f32[6,16,4]{1,0,2:T(8,128)S(1)}, f32[6,16,4]{1,0,2:T(8,128)S(1)}, u32[]{:S(2)}, u32[]{:S(2)}) collective-permute-start(f32[6,16,4]{1,0,2:T(8,128)S(1)} %copy.200), channel_id=1, source_target_pairs={{0,8},{8,16},{16,24},{24,32},{32,40},{40,48},{48,56},{56,64},{64,7... | collective-permute-start | bytes 4616 | tf_op jit(solution)/shard_map/ppermute | solution.py:15
  121.1 21.8 %collective-permute-start.11 = (f32[6,16,4]{1,0,2:T(8,128)S(1)}, f32[6,16,4]{1,0,2:T(8,128)S(1)}, u32[]{:S(2)}, u32[]{:S(2)}) collective-permute-start(f32[6,16,4]{1,0,2:T(8,128)S(1)} %copy.200), channel_id=1, source_target_pairs={{0,264},{8,272},{16,280},{24,288},{32,296},{40,304},{48,312},{56,3... | collective-permute-start | bytes 4616 | tf_op jit(solution)/shard_map/ppermute | solution.py:15
  127.2 11.4 %collective-permute-start.10 = (f32[6,16,4]{1,0,2:T(8,128)S(1)}, f32[6,16,4]{1,0,2:T(8,128)S(1)}, u32[]{:S(2)}, u32[]{:S(2)}) collective-permute-start(f32[6,16,4]{1,0,2:T(8,128)S(1)} %copy.200), channel_id=1, source_target_pairs={{0,504},{8,0},{16,8},{24,16},{32,24},{40,32},{48,40},{56,48},{64,5... | collective-permute-start | bytes 4616 | tf_op jit(solution)/shard_map/ppermute | solution.py:15
  129.8 13.1 %collective-permute-start.9 = (f32[6,16,4]{1,0,2:T(8,128)S(1)}, f32[6,16,4]{1,0,2:T(8,128)S(1)}, u32[]{:S(2)}, u32[]{:S(2)}) collective-permute-start(f32[6,16,4]{1,0,2:T(8,128)S(1)} %copy.200), channel_id=1, source_target_pairs={{0,248},{8,256},{16,264},{24,272},{32,280},{40,288},{48,296},{56,3... | collective-permute-start | bytes 4616 | tf_op jit(solution)/shard_map/ppermute | solution.py:15
  136.3 7.3 %collective-permute-start.14 = (f32[6,16,1]{1,0,2:T(8,128)S(1)}, f32[6,16,1]{1,0,2:T(8,128)S(1)}, u32[]{:S(2)}, u32[]{:S(2)}) collective-permute-start(f32[6,16,1]{1,0,2:T(8,128)S(1)} %get-tuple-element.23), channel_id=1, source_target_pairs={{0,1},{1,2},{2,3},{3,4},{4,5},{5,6},{6,7},{7,0},{8,9},{9,10},{10,1... | collective-permute-start | bytes 1160 | tf_op jit(solution)/shard_map/ppermute | solution.py:15
  138.6 5.0 %collective-permute-start.13 = (f32[6,16,1]{1,0,2:T(8,128)S(1)}, f32[6,16,1]{1,0,2:T(8,128)S(1)}, u32[]{:S(2)}, u32[]{:S(2)}) collective-permute-start(f32[6,16,1]{1,0,2:T(8,128)S(1)} %get-tuple-element.24), channel_id=1, source_target_pairs={{0,7},{1,0},{2,1},{3,2},{4,3},{5,4},{6,5},{7,6},{8,15},{9,8},{10,9... | collective-permute-start | bytes 1160 | tf_op jit(solution)/shard_map/ppermute | solution.py:15
where the time goes:
time: 148 us; the launch traced here: 147 us
  starting transfers between devices  70.2 us (47%)
  blocking collectives  50.5 us (34%)
  matrix products  8.75 us (6%)
  local copies, waits for them, and re-layouts  5.82 us (4%)
  other arithmetic  5.57 us (4%)
  waiting for transfers between devices  5.38 us (4%)
    ppermute x15, starting transfers between devices, shifted(): lax.ppermute(value, axis, [(i, (i + by) % peers) for i in range(peers)])  70.2 us
    all_to_all x2, blocking collectives, sent_and_summed(): lax.all_to_all(parts, axis, split_axis=0, concat_axis=0, tiled=True)  25.6 us
    all_to_all x2, blocking collectives, copy_for_each(): return lax.all_to_all(copies, axis, split_axis=0, concat_axis=0, tiled=True)  24.9 us
    ppermute x15, waiting for transfers between devices, shifted(): lax.ppermute(value, axis, [(i, (i + by) % peers) for i in range(peers)])  5.38 us
    dot_general x6, matrix products, body(): jnp.einsum('ksm,rsm->krs', masked_modes[which_face], multipliers, precisi...  3.6 us
  transfers between devices with their start and end apart: 15, of which 2 were waited for; matrix products, arithmetic and copies ran while one was open for 0% of the time, Pallas kernels for 0%

commit v1 on v0

v1 whole, which is shorter than its diff:
```python
import functools

import jax
import jax.numpy as jnp
from jax import lax
from jax.experimental import pallas as pl
from jax.experimental.pallas import tpu as pltpu
from jax.sharding import PartitionSpec as P

MODES = 6
NFACE = 6
PAD = 8
BLOCK = 32
F32 = jnp.float32
BF16 = jnp.bfloat16


def split(value):
    high = value.astype(BF16)
    return high, (value - high.astype(F32)).astype(BF16)


def dot3(value, high, low, transposed=False):
    rows = value.shape[0]
    first, second = split(value)
    dims = (((1,), (1 if transposed else 0,)), ((), ()))
    both = jnp.concatenate([first, second], axis=0)
    top = lax.dot_general(both, high, dims, preferred_element_type=F32)
    rest = lax.dot_general(first, low, dims, preferred_element_type=F32)
    return top[:rows] + top[rows:] + rest


def swap_blocks(parts):
    block = lax.broadcasted_iota(jnp.int32, parts[0].shape, 1) // BLOCK
    turned = [
        [part if by == 0 else pltpu.roll(part, BLOCK * by, 1) for by in range(4)] for part in parts
    ]
    out = []
    for q in range(4):
        value = turned[3][(3 - q) % 4]
        for d in (2, 1, 0):
            value = jnp.where(block == d, turned[d][(d - q) % 4], value)
        out.append(value)
    return out


def row_blocks(value):
    return [value[4 * q : 4 * q + 4] for q in range(4)]


def kernel(
    mult_h, own_h, near_h, face_h, list_h, coarse_h, out_h,
    mult, own, near, face, nlist, coarse, result,
    m_high, m_low, c_high, c_low,
    halo_out, halo_in, group, part_out, part_in, column, panel,
    amp_out, amp_in, side_out, side_in,
    load_sem, store_sem, send_sem, recv_sem,
):
    sub, crs = lax.axis_index("sub"), lax.axis_index("crs")
    y, xc = sub // 8, lax.rem(sub, 8)
    half, second = sub // 32, lax.rem(sub, 32)
    x_sub = lax.rem(sub + 32, 64)
    up_sub = half * 32 + lax.rem(second + 1, 32)
    down_sub = half * 32 + lax.rem(second + 31, 32)

    barrier = pltpu.get_barrier_semaphore()
    greeted = [(up_sub, crs), (down_sub, crs)]
    for k in range(1, 8):
        greeted.append((lax.rem(sub + 8 * k, 64), crs))
        greeted.append((sub, lax.rem(crs + k, 8)))
        greeted.append((y * 8 + lax.rem(xc + k, 8), crs))
    for peer in greeted:
        pl.semaphore_signal(barrier, inc=1, device_id=peer, device_id_type=pl.DeviceIdType.MESH)

    list_row = pl.multiple_of(sub * 32 + crs // 2 * 8, 8)
    loads = [
        pltpu.make_async_copy(src, dst, load_sem.at[i])
        for i, (src, dst) in enumerate(
            [
                (list_h.at[pl.ds(list_row, 8)], nlist),
                (face_h, face),
                (near_h, near),
                (own_h, own),
                (mult_h, mult),
                (coarse_h, coarse),
            ]
        )
    ]
    for load in loads:
        load.start()

    def send(src, dst, stage, peer):
        copy = pltpu.make_async_remote_copy(
            src_ref=src,
            dst_ref=dst,
            send_sem=send_sem.at[stage],
            recv_sem=recv_sem.at[stage],
            device_id=peer,
            device_id_type=pl.DeviceIdType.MESH,
        )
        copy.start()

    def landed(ref, stage):
        pltpu.make_async_copy(ref, ref, recv_sem.at[stage]).wait()

    def left(ref, stage):
        pltpu.make_async_copy(ref, ref, send_sem.at[stage]).wait()

    for i in range(4):
        loads[i].wait()
    rows = jnp.where(lax.rem(crs, 2) == 0, nlist[0:4, :], nlist[4:8, :])
    faces = face[...]
    across = jnp.zeros(faces.shape, jnp.int32)
    for which in range(NFACE):
        across = jnp.where(faces == which, rows[:, which : which + 1], across)
    third = crs * 4 + lax.broadcasted_iota(jnp.int32, faces.shape, 0)

    def place(group_index, c):
        return group_index * 32 + c

    targets = [
        place(x_sub, third),
        place(up_sub, third),
        place(down_sub, third),
        place(sub, lax.rem(third + 1, 32)),
        place(sub, lax.rem(third + 31, 32)),
    ]
    masks = [(across == target).astype(F32) for target in targets]
    blank = jnp.zeros((PAD, faces.shape[1]), F32)
    spare = jnp.zeros((PAD - MODES, faces.shape[1]), F32)
    loads[4].wait()
    sums = jnp.zeros((16, 160), F32)
    for j in range(4):
        near_j = jnp.concatenate([near[:, j, :], spare], axis=0)
        own_j = jnp.concatenate([own[:, j, :], spare], axis=0)
        seen = [near_j * mask[j : j + 1, :] for mask in masks]
        blocks = [blank] * 20
        blocks[j] = own_j
        for d in range(3):
            blocks[4 * (d + 1) + j] = seen[d]
        blocks[j + 1 if j < 3 else 16] = seen[3]
        blocks[j - 1 if j > 0 else 19] = seen[4]
        high, low = split(jnp.concatenate(blocks, axis=0))
        m_high[j] = high
        m_low[j] = low
        sums += dot3(mult[:, j, :], high, low, transposed=True)

    packed = swap_blocks(row_blocks(sums[:, :128]))
    edge = jnp.concatenate([sums[:, 128:], jnp.zeros((16, 96), F32)], axis=1)
    block4 = lax.broadcasted_iota(jnp.int32, (4, 128), 1)
    edges = row_blocks(edge)
    packed_edge = edges[0]
    for q in range(1, 4):
        packed_edge = jnp.where(block4 // BLOCK == q, pltpu.roll(edges[q], BLOCK * q, 1), packed_edge)
    for d in range(3):
        halo_out[d] = packed[d + 1]
    halo_out[3] = packed_edge

    pl.semaphore_wait(barrier, len(greeted))

    send(halo_out.at[0], halo_in.at[0], 0, (x_sub, crs))
    send(halo_out.at[1], halo_in.at[1], 0, (up_sub, crs))
    send(halo_out.at[2], halo_in.at[2], 0, (down_sub, crs))
    send(halo_out.at[3], halo_in.at[3], 0, (sub, lax.rem(crs + 1, 8)))
    send(halo_out.at[3], halo_in.at[4], 0, (sub, lax.rem(crs + 7, 8)))

    loads[5].wait()
    space = jnp.zeros((PAD - MODES, coarse.shape[1]), F32)
    for c in range(8):
        pieces = []
        for j in range(4):
            at = 24 * c + 6 * j
            pieces += [coarse[at : at + MODES, :], space]
        high, low = split(jnp.concatenate(pieces, axis=0))
        c_high[BLOCK * c : BLOCK * c + BLOCK, :] = high
        c_low[BLOCK * c : BLOCK * c + BLOCK, :] = low

    landed(halo_in, 0)
    lane = lax.rem(block4, BLOCK)
    chunk = packed[0] + halo_in[0] + halo_in[1] + halo_in[2]
    chunk += jnp.where(lane < PAD, halo_in[3], 0.0) + jnp.where(lane >= 24, halo_in[4], 0.0)
    group[crs] = chunk
    for k in range(1, 8):
        send(group.at[crs], group.at[crs], 1, (sub, lax.rem(crs + k, 8)))
    landed(group.at[pl.ds(0, 7)], 1)

    halves = []
    for h in range(2):
        halves.append(jnp.concatenate(swap_blocks([group[4 * h + d] for d in range(4)]), axis=0))
    rhs = jnp.concatenate(halves, axis=1)
    partial = dot3(rhs, c_high[...], c_low[...])
    for i in range(8):
        h, g = i // 4, i % 4
        part_out[i] = partial[8 * h : 8 * h + 8, 384 * g : 384 * g + 384]
    for k in range(1, 8):
        peer = lax.rem(xc + k, 8)
        send(part_out.at[peer], part_in.at[xc], 2, (y * 8 + peer, crs))
    part_in[xc] = part_out[xc]
    landed(part_in.at[pl.ds(0, 7)], 2)

    def total(ref):
        value = ref[0]
        for i in range(1, 8):
            value = value + ref[i]
        return value

    column[y] = total(part_in)
    for k in range(1, 8):
        send(column.at[y], column.at[y], 3, (lax.rem(y + k, 8) * 8 + xc, crs))
    landed(column.at[pl.ds(0, 7)], 3)
    panel[xc] = total(column)
    for k in range(1, 8):
        send(panel.at[xc], panel.at[xc], 4, (y * 8 + lax.rem(xc + k, 8), crs))
    landed(panel.at[pl.ds(0, 7)], 4)

    whole = jnp.concatenate(
        [jnp.concatenate([panel[4 * h + g] for g in range(4)], axis=1) for h in range(2)], axis=0
    )
    amps = dot3(whole, c_high[...], c_low[...], transposed=True)
    ready = []
    for h in range(2):
        ready += swap_blocks(row_blocks(amps[:, 128 * h : 128 * h + 128]))
    for c in range(8):
        side_out[c] = ready[c]
        rim = jnp.where(lane < PAD, ready[(c + 1) % 8], ready[(c + 7) % 8])
        amp_out[c] = jnp.concatenate([ready[c], rim], axis=0)
    for k in range(8):
        send(side_out.at[k], side_in.at[0, crs], 6, (x_sub, k))
        send(side_out.at[k], side_in.at[2, crs], 6, (up_sub, k))
        send(side_out.at[k], side_in.at[1, crs], 6, (down_sub, k))
    for k in range(1, 8):
        peer = lax.rem(crs + k, 8)
        send(amp_out.at[peer], amp_in.at[crs], 5, (sub, peer))
    amp_in[crs] = amp_out[crs]
    landed(amp_in.at[pl.ds(0, 7)], 5)
    landed(side_in, 6)

    mine = total(amp_in)
    sides = [total(side_in.at[d]) for d in range(3)]
    main = jnp.concatenate(swap_blocks([mine[0:4]] + sides), axis=0)
    rims = [mine[4:8]] + [pltpu.roll(mine[4:8], 128 - BLOCK * q, 1) for q in range(1, 4)]
    rim = jnp.concatenate(rims, axis=0)[:, :BLOCK]
    lhs = jnp.concatenate([main, rim], axis=1)
    for j in range(4):
        applied = dot3(lhs, m_high[j], m_low[j])
        result[:, j, :] = mult[:, j, :] - applied
    store = pltpu.make_async_copy(result, out_h, store_sem)
    store.start()
    left(halo_in, 0)
    left(group.at[pl.ds(0, 7)], 1)
    left(part_in.at[pl.ds(0, 7)], 2)
    left(column.at[pl.ds(0, 7)], 3)
    left(panel.at[pl.ds(0, 7)], 4)
    left(amp_in.at[pl.ds(0, 7)], 5)
    left(side_in, 6)
    store.wait()


def body(multipliers, own_modes, neighbour_modes, face_index, neighbour_list, coarse_factor):
    anywhere = pl.BlockSpec(memory_space=pl.ANY)
    rows, columns = coarse_factor.shape
    width = face_index.shape[1]
    return pl.pallas_call(
        kernel,
        out_shape=jax.ShapeDtypeStruct(multipliers.shape, F32),
        in_specs=[anywhere] * 6,
        out_specs=anywhere,
        scratch_shapes=[
            pltpu.VMEM(multipliers.shape, F32),
            pltpu.VMEM(own_modes.shape, F32),
            pltpu.VMEM(own_modes.shape, F32),
            pltpu.VMEM(face_index.shape, jnp.int32),
            pltpu.VMEM((8, NFACE), jnp.int32),
            pltpu.VMEM((rows, columns), F32),
            pltpu.VMEM(multipliers.shape, F32),
            pltpu.VMEM((4, 160, width), BF16),
            pltpu.VMEM((4, 160, width), BF16),
            pltpu.VMEM((256, columns), BF16),
            pltpu.VMEM((256, columns), BF16),
            pltpu.VMEM((4, 4, 128), F32),
            pltpu.VMEM((5, 4, 128), F32),
            pltpu.VMEM((8, 4, 128), F32),
            pltpu.VMEM((8, 8, 384), F32),
            pltpu.VMEM((8, 8, 384), F32),
            pltpu.VMEM((8, 8, 384), F32),
            pltpu.VMEM((8, 8, 384), F32),
            pltpu.VMEM((8, 8, 128), F32),
            pltpu.VMEM((8, 8, 128), F32),
            pltpu.VMEM((8, 4, 128), F32),
            pltpu.VMEM((3, 8, 4, 128), F32),
            pltpu.SemaphoreType.DMA((6,)),
            pltpu.SemaphoreType.DMA,
            pltpu.SemaphoreType.DMA((7,)),
            pltpu.SemaphoreType.DMA((7,)),
        ],
        compiler_params=pltpu.CompilerParams(collective_id=0, has_side_effects=True),
    )(multipliers, own_modes, neighbour_modes, face_index, neighbour_list, coarse_factor)


def solution(mesh):
    placed = (
        P(None, ("sub", "crs"), None),
        P(None, ("sub", "crs"), None),
        P(None, ("sub", "crs"), None),
        P(("sub", "crs"), None),
        P(),
        P("sub", "crs"),
    )
    return jax.shard_map(
        body, mesh=mesh, in_specs=placed, out_specs=P(None, ("sub", "crs"), None), check_vma=False
    )
```

time: 148 us -> 50.3 us (0.34)
  starting transfers between devices: 70.2 us -> 0 us
  blocking collectives: 50.5 us -> 0 us
  Pallas kernels: 0 us -> 46.3 us
  matrix products: 8.75 us -> 0 us
  other arithmetic: 5.57 us -> 0 us
  waiting for transfers between devices: 5.38 us -> 0 us
  local copies, waits for them, and re-layouts: 5.82 us -> 3.77 us
    ppermute x15 -> x0, starting transfers between devices: 70.2 us -> none  [shifted(): lax.ppermute(value, axis, [(i, (i + by) % peers) for i in range(peers)])]
    all_to_all x4 -> x0, blocking collectives: 50.5 us -> none  [the longest x2 25.6 us: sent_and_summed(): lax.all_to_all(parts, axis, split_axis=0, concat_axis=0, tiled=True)]
    pallas_call x0 -> x1, Pallas kernels: none -> 46.3 us  [body(): pl.pallas_call(kernel, out_shape=jax.ShapeDtypeStruct(multipliers.shape,...]
    dot_general x18 -> x0, matrix products: 8.75 us -> none  [the longest x6 3.6 us: body(): jnp.einsum('ksm,rsm->krs', masked_modes[which_face], multipliers, precisi...]
    ppermute x15 -> x0, waiting for transfers between devices: 5.38 us -> none  [shifted(): lax.ppermute(value, axis, [(i, (i + by) % peers) for i in range(peers)])]
    all_to_all x4 -> x0, other arithmetic: 3.11 us -> none  [the longest x2 1.55 us: sent_and_summed(): lax.all_to_all(parts, axis, split_axis=0, concat_axis=0, tiled=True)]
    unnamed x24 -> x2, local copies, waits for them, and re-layouts: 2 us -> 3.77 us
  transfers between devices with their start and end apart: 15 -> 0, of which waited for: 2 -> 0; matrix products, arithmetic and copies ran while one was open for 0% -> 0% of each run, Pallas kernels for 0% -> 0%
where the time goes in v1:
time: 50.3 us; the launch traced here: 50.1 us
  Pallas kernels  46.3 us (92%)
  local copies, waits for them, and re-layouts  3.77 us (7%)
    pallas_call x1, Pallas kernels, body(): pl.pallas_call(kernel, out_shape=jax.ShapeDtypeStruct(multipliers.shape,...  46.3 us
    unnamed x2, local copies, waits for them, and re-layouts  3.77 us

profile of v1, /device:TPU:1, one launch (start us, length us, event | category | flops | bytes accessed | tf_op | source)
XLA Modules:
  0.0 50.1 jit_solution(2566596865086386833)
XLA Ops:
  0.0 2.2 %copy.7.list_h = s32[2048,6]{1,0:T(8,128)} copy(s32[2048,6]{0,1:T(8,128)} %param.10) | data formatting | bytes 98304 | tf_op args[4]
  2.2 46.3 %shard_map.64 = f32[16,4,512]{2,1,0:T(4,128)} custom-call(f32[16,4,512]{2,1,0:T(4,128)} %mult_h.1, f32[6,4,512]{2,1,0:T(4,128)} %own_h.1, f32[6,4,512]{2,1,0:T(4,128)} %near_h.1, s32[4,512]{1,0:T(4,128)} %face_h.1, s32[2048,6]{1,0:T(8,128)} %copy.7.list_h, f32[192,1536]{1,0:T(8,128)} %coarse_h.1), custom_call_target="tpu_custom_call" | custom-call | tf_op jit(solution)/shard_map/pallas_call | solution.py:263
  48.5 1.6 %copy.9 = f32[16,4,512]{2,1,0:T(4,128)} copy(f32[16,4,512]{2,1,0:T(4,128)} %shard_map.64) | data formatting | bytes 262144

commit v2 on v1

v2 whole, which is shorter than its diff:
```python
import functools

import jax
import jax.numpy as jnp
from jax import lax
from jax.experimental import pallas as pl
from jax.experimental.pallas import tpu as pltpu
from jax.sharding import PartitionSpec as P

MODES = 6
NFACE = 6
BLOCK = 32
F32 = jnp.float32
BF16 = jnp.bfloat16


def split(value):
    high = value.astype(BF16)
    return high, (value - high.astype(F32)).astype(BF16)


def dot3(value, high, low, transposed=False):
    rows = value.shape[0]
    first, second = split(value)
    dims = (((1,), (1 if transposed else 0,)), ((), ()))
    both = jnp.concatenate([first, second], axis=0)
    top = lax.dot_general(both, high, dims, preferred_element_type=F32)
    rest = lax.dot_general(first, low, dims, preferred_element_type=F32)
    return top[:rows] + top[rows:] + rest


def swap_blocks(parts):
    block = lax.broadcasted_iota(jnp.int32, parts[0].shape, 1) // BLOCK
    turned = [
        [part if by == 0 else pltpu.roll(part, BLOCK * by, 1) for by in range(4)] for part in parts
    ]
    out = []
    for q in range(4):
        value = turned[3][(3 - q) % 4]
        for d in (2, 1, 0):
            value = jnp.where(block == d, turned[d][(d - q) % 4], value)
        out.append(value)
    return out


def row_blocks(value):
    return [value[4 * q : 4 * q + 4] for q in range(4)]


def all_sends(n):
    return sorted(range(1, n), key=lambda k: -min(k, n - k))


def kernel(
    mult_h, own_h, near_h, face_h, list_h, coarse_h, result,
    local, face, nlist, coarse,
    m_high, m_low, c_high, c_low, t_high, t_low,
    halo_out, halo_in, group, part_out, part_in, column, panel,
    amp_out, amp_in, side_out, side_in, early,
    load_sem, send_sem, recv_sem, ready_sem,
):
    sub, crs = lax.axis_index("sub"), lax.axis_index("crs")
    y, xc = sub // 8, lax.rem(sub, 8)
    half, second = sub // 32, lax.rem(sub, 32)
    x_sub = lax.rem(sub + 32, 64)
    up_sub = half * 32 + lax.rem(second + 1, 32)
    down_sub = half * 32 + lax.rem(second + 31, 32)
    ring = all_sends(8)

    barrier = pltpu.get_barrier_semaphore()

    def greet(peer):
        pl.semaphore_signal(barrier, inc=1, device_id=peer, device_id_type=pl.DeviceIdType.MESH)

    along_z = [(k, lax.rem(crs + k, 8)) for k in (4, 3, 5, 2, 6)]
    along_y = [(k, lax.rem(y + k, 8)) for k in (3, 5, 2, 6, 1, 7)]
    chip, core = xc // 2, lax.rem(xc, 2)
    along_x = [
        (k, lax.rem(chip + k, 4) * 2 + (core if same else 1 - core))
        for k, same in ((2, 1), (2, 0), (1, 1), (1, 0), (3, 1), (3, 0), (0, 0))
    ]
    classes = [
        (along_z, crs, ready_sem.at[0], lambda at: (sub, at)),
        (along_y, y, ready_sem.at[1], lambda at: (at * 8 + xc, crs)),
        (along_x, xc, ready_sem.at[2], lambda at: (y * 8 + at, crs)),
    ]
    greet((x_sub, crs))
    greet((up_sub, crs))
    greet((down_sub, crs))
    greet((sub, lax.rem(crs + 1, 8)))
    greet((sub, lax.rem(crs + 7, 8)))

    list_at = pl.multiple_of(sub // 4 * 128, 128)
    loads = [
        (list_h, nlist, 0),
        (face_h, face, 1),
        (near_h, local.at[pl.ds(MODES, MODES)], 2),
        (own_h, local.at[pl.ds(0, MODES)], 2),
        (mult_h, local.at[pl.ds(2 * MODES, 16)], 2),
    ]
    for src, dst, i in loads:
        pltpu.make_async_copy(src, dst, load_sem.at[i]).start()
    expected = jnp.int32(5)
    for peers, mine, _, where in classes:
        for _, at in peers:
            pl.when(at > mine)(functools.partial(lambda where, at: greet(where(at)), where, at))
            expected += jnp.where(at < mine, 1, 0)
    pltpu.make_async_copy(coarse_h, coarse, load_sem.at[3]).start()

    def tell(ready, where, at):
        pl.semaphore_signal(
            ready, inc=1, device_id=where(at), device_id_type=pl.DeviceIdType.MESH
        )

    def heard(which):
        peers, mine, ready, _ = classes[which]
        higher = jnp.int32(0)
        for _, at in peers:
            higher += jnp.where(at > mine, 1, 0)
        pl.when(higher > 0)(lambda: pl.semaphore_wait(ready, higher))

    def send(src, dst, stage, peer):
        copy = pltpu.make_async_remote_copy(
            src_ref=src,
            dst_ref=dst,
            send_sem=send_sem,
            recv_sem=recv_sem.at[stage],
            device_id=peer,
            device_id_type=pl.DeviceIdType.MESH,
        )
        copy.start()

    def loaded(ref, which):
        pltpu.make_async_copy(ref, ref, load_sem.at[which]).wait()

    def landed(ref, stage):
        pltpu.make_async_copy(ref, ref, recv_sem.at[stage]).wait()

    loaded(nlist, 0)
    loaded(face, 1)
    shift = lax.rem(sub, 4) * 32 + crs * 4
    lists = pltpu.roll(nlist[:, pl.ds(list_at, 128)], lax.rem(128 - shift, 128), 1).astype(F32)
    faces = face[...]
    width = faces.shape[1]
    which = lax.broadcasted_iota(jnp.int32, (NFACE, width), 0)
    across = []
    for j in range(4):
        named = jnp.where(faces[j : j + 1, :] == which, lists[:, j : j + 1], 0.0)
        across.append(jnp.sum(named, axis=0, keepdims=True))
    across = jnp.concatenate(across, axis=0).astype(jnp.int32)
    third = crs * 4 + lax.broadcasted_iota(jnp.int32, faces.shape, 0)
    targets = [
        x_sub * 32 + third,
        up_sub * 32 + third,
        down_sub * 32 + third,
        sub * 32 + lax.rem(third + 1, 32),
        sub * 32 + lax.rem(third + 31, 32),
    ]
    loaded(local, 2)
    blank = jnp.zeros((8, width), F32)
    stack = [local[k] for k in range(MODES)] + [blank]
    for target in targets:
        hit = across == target
        stack += [jnp.where(hit, local[MODES + k], 0.0) for k in range(MODES)] + [blank]
    high, low = split(jnp.concatenate(stack, axis=0))
    m_high[...] = high
    m_low[...] = low
    values = jnp.concatenate([local[2 * MODES + r] for r in range(16)], axis=0)
    every = dot3(values, high, low, transposed=True)
    mine_rows = lax.broadcasted_iota(jnp.int32, every.shape, 0) % 4
    mine_lanes = lax.broadcasted_iota(jnp.int32, every.shape, 1) % 4
    same = mine_rows == mine_lanes
    sums = jnp.sum(jnp.where(same, every, 0.0).reshape(16, 4, 192), axis=1)

    packed = swap_blocks(row_blocks(sums[:, :128]))
    tail = jnp.concatenate([sums[:, 128:], jnp.zeros((16, 64), F32)], axis=1)
    above, below = swap_blocks(row_blocks(tail))[:2]
    place = lax.rem(lax.broadcasted_iota(jnp.int32, (4, 128), 1), 4)
    for d in range(3):
        halo_out[d] = packed[d + 1]
    crossing = jnp.where(place == 3, pltpu.roll(below, 3, 1), 0.0)
    halo_out[3] = jnp.where(place == 0, pltpu.roll(above, 125, 1), crossing)

    pl.semaphore_wait(barrier, expected)
    send(halo_out.at[0], halo_in.at[0], 0, (x_sub, crs))
    send(halo_out.at[1], halo_in.at[1], 0, (up_sub, crs))
    send(halo_out.at[2], halo_in.at[2], 0, (down_sub, crs))
    send(halo_out.at[3], halo_in.at[3], 0, (sub, lax.rem(crs + 1, 8)))
    send(halo_out.at[3], halo_in.at[4], 0, (sub, lax.rem(crs + 7, 8)))
    for peers, mine, ready, where in classes:
        for _, at in peers:
            pl.when(at < mine)(functools.partial(tell, ready, where, at))

    chunk = packed[0] + jnp.where(place > 0, pltpu.roll(above, 1, 1), 0.0)
    chunk += jnp.where(place < 3, pltpu.roll(below, 127, 1), 0.0)

    space = jnp.zeros((8, 128), F32)
    loaded(coarse, 3)
    for g in range(12):
        for c in range(8):
            lanes = slice(128 * g, 128 * g + 128)
            at = [24 * c + 6 * j + k for k in range(MODES) for j in range(4)]
            rows = [coarse[i : i + 1, lanes] for i in at]
            high, low = split(jnp.concatenate(rows + [space], axis=0))
            c_high[BLOCK * c : BLOCK * c + BLOCK, 128 * g : 128 * g + 128] = high
            c_low[BLOCK * c : BLOCK * c + BLOCK, 128 * g : 128 * g + 128] = low

    landed(halo_in, 0)
    chunk += halo_in[0] + halo_in[1] + halo_in[2]
    chunk += jnp.where(place == 0, halo_in[3], 0.0) + jnp.where(place == 3, halo_in[4], 0.0)
    group[crs] = chunk
    for k in (1, 7):
        send(group.at[crs], group.at[crs], 1, (sub, lax.rem(crs + k, 8)))
    heard(0)
    for k, at in along_z:
        send(group.at[crs], group.at[crs], 1 if k in (2, 6) else 6, (sub, at))
    for h in range(2):
        t_high[:, 128 * h : 128 * h + 128] = c_high[128 * h : 128 * h + 128, :].T
        t_low[:, 128 * h : 128 * h + 128] = c_low[128 * h : 128 * h + 128, :].T

    def gathered(wave):
        blocks = [lax.rem(crs + k, 8) for k in wave]
        chunks = [group[c] for c in blocks]
        chunks += [jnp.zeros((4, 128), F32)] * (-len(wave) % 4)
        lhs = [
            jnp.concatenate(swap_blocks(chunks[i : i + 4]), axis=0)
            for i in range(0, len(chunks), 4)
        ]
        lhs = jnp.concatenate(lhs, axis=1)[:, : BLOCK * len(wave)]
        return lhs, [pl.ds(pl.multiple_of(BLOCK * c, BLOCK), BLOCK) for c in blocks]

    def product(lhs, at, lanes):
        high = jnp.concatenate([c_high[rows, lanes] for rows in at], axis=0)
        low = jnp.concatenate([c_low[rows, lanes] for rows in at], axis=0)
        return dot3(lhs, high, low)

    heard(2)
    landed(group.at[pl.ds(0, 4)], 1)
    early[...] = product(*gathered((0, 1, 7, 2, 6)), slice(None))
    landed(group.at[pl.ds(0, 3)], 6)
    late = gathered((3, 5, 4))
    side = lax.rem(chip, 2)
    for step, which in enumerate((side, 1 - side)):
        lanes = pl.ds(pl.multiple_of(which * 768, 768), 768)
        partial = early[:, lanes] + product(*late, lanes)
        for h in range(2):
            for g in range(2):
                piece = partial[8 * h : 8 * h + 8, 384 * g : 384 * g + 384]
                part_out[4 * h + 2 * which + g] = piece
        for k, peer in along_x:
            if (k in (0, 2)) == (step == 0):
                send(part_out.at[peer], part_in.at[xc], 2, (y * 8 + peer, crs))
    part_in[xc] = part_out[xc]
    heard(1)
    landed(part_in.at[pl.ds(0, 7)], 2)

    def total(ref):
        value = ref[0]
        for i in range(1, 8):
            value = value + ref[i]
        return value

    column[y] = total(part_in)
    send(column.at[y], column.at[y], 3, (x_sub, crs))
    for _, at in along_y:
        send(column.at[y], column.at[y], 3, (at * 8 + xc, crs))
    landed(column.at[pl.ds(0, 7)], 3)
    panel[xc] = total(column)
    for _, peer in along_x:
        send(panel.at[xc], panel.at[xc], 4, (y * 8 + peer, crs))
    landed(panel.at[pl.ds(0, 7)], 4)

    whole = jnp.concatenate(
        [jnp.concatenate([panel[4 * h + g] for g in range(4)], axis=1) for h in range(2)], axis=0
    )
    ready = []
    for h in range(2):
        lanes = slice(128 * h, 128 * h + 128)
        ready += swap_blocks(row_blocks(dot3(whole, t_high[:, lanes], t_low[:, lanes])))
        for c in range(4 * h, 4 * h + 4):
            side_out[c] = ready[c]
        for c in range(4 * h, 4 * h + 4):
            send(side_out.at[c], side_in.at[0, crs], 7, (x_sub, c))
        for c in range(4 * h, 4 * h + 4):
            send(side_out.at[c], side_in.at[2, crs], 7, (up_sub, c))
            send(side_out.at[c], side_in.at[1, crs], 7, (down_sub, c))
    for c in range(8):
        rim = jnp.where(place == 0, ready[(c + 1) % 8], ready[(c + 7) % 8])
        amp_out[c] = jnp.concatenate([ready[c], rim], axis=0)
    for k in ring:
        peer = lax.rem(crs + k, 8)
        send(amp_out.at[peer], amp_in.at[crs], 5, (sub, peer))
    amp_in[crs] = amp_out[crs]
    def applied(parts, rows):
        parts = parts + [jnp.zeros((4, 128), F32)]
        lhs = jnp.concatenate(swap_blocks(parts), axis=0)[:, :96]
        lhs = jnp.broadcast_to(lhs[:, None, :], (16, 4, 96)).reshape(64, 96)
        high = jnp.concatenate([m_high[at, :] for at in rows], axis=0)
        low = jnp.concatenate([m_low[at, :] for at in rows], axis=0)
        return dot3(jnp.where(same[:, :96], lhs, 0.0), high, low)

    landed(amp_in.at[pl.ds(0, 7)], 5)
    mine = total(amp_in)
    centre, rim = mine[0:4], mine[4:8]
    above = jnp.where(place < 3, pltpu.roll(centre, 127, 1), pltpu.roll(rim, 3, 1))
    below = jnp.where(place > 0, pltpu.roll(centre, 1, 1), pltpu.roll(rim, 125, 1))
    inner = applied([centre, above, below], (slice(0, 32), slice(128, 192)))
    for r in range(16):
        result[r] = local[2 * MODES + r] - inner[4 * r : 4 * r + 4]
    landed(side_in, 7)
    outer = applied([total(side_in.at[d]) for d in range(3)], (slice(32, 128),))
    for r in range(16):
        result[r] -= outer[4 * r : 4 * r + 4]
    everything = t_high.at[pl.ds(0, 704)]
    pltpu.make_async_copy(everything, everything, send_sem).wait()


def body(multipliers, own_modes, neighbour_modes, face_index, neighbour_list, coarse_factor):
    anywhere = pl.BlockSpec(memory_space=pltpu.HBM)
    rows, columns = coarse_factor.shape
    width = face_index.shape[1]
    return pl.pallas_call(
        kernel,
        out_shape=pltpu.VMEM(multipliers.shape, F32),
        in_specs=[anywhere] * 6,
        out_specs=pl.BlockSpec(memory_space=pltpu.VMEM),
        scratch_shapes=[
            pltpu.VMEM((2 * MODES + 16, 4, width), F32),
            pltpu.VMEM(face_index.shape, jnp.int32),
            pltpu.VMEM((NFACE, 2048), jnp.int32),
            pltpu.VMEM((rows, columns), F32),
            pltpu.VMEM((192, width), BF16),
            pltpu.VMEM((192, width), BF16),
            pltpu.VMEM((256, columns), BF16),
            pltpu.VMEM((256, columns), BF16),
            pltpu.VMEM((columns, 256), BF16),
            pltpu.VMEM((columns, 256), BF16),
            pltpu.VMEM((4, 4, 128), F32),
            pltpu.VMEM((5, 4, 128), F32),
            pltpu.VMEM((8, 4, 128), F32),
            pltpu.VMEM((8, 8, 384), F32),
            pltpu.VMEM((8, 8, 384), F32),
            pltpu.VMEM((8, 8, 384), F32),
            pltpu.VMEM((8, 8, 384), F32),
            pltpu.VMEM((8, 8, 128), F32),
            pltpu.VMEM((8, 8, 128), F32),
            pltpu.VMEM((8, 4, 128), F32),
            pltpu.VMEM((3, 8, 4, 128), F32),
            pltpu.VMEM((16, columns), F32),
            pltpu.SemaphoreType.DMA((4,)),
            pltpu.SemaphoreType.DMA,
            pltpu.SemaphoreType.DMA((8,)),
            pltpu.SemaphoreType.REGULAR((3,)),
        ],
        compiler_params=pltpu.CompilerParams(collective_id=0, has_side_effects=True),
    )(multipliers, own_modes, neighbour_modes, face_index, neighbour_list.T, coarse_factor)


def solution(mesh):
    placed = (
        P(None, ("sub", "crs"), None),
        P(None, ("sub", "crs"), None),
        P(None, ("sub", "crs"), None),
        P(("sub", "crs"), None),
        P(),
        P("sub", "crs"),
    )
    return jax.shard_map(
        body, mesh=mesh, in_specs=placed, out_specs=P(None, ("sub", "crs"), None), check_vma=False
    )
```

time: 50.3 us -> 43.7 us (0.87)
  Pallas kernels: 46.3 us -> 42.9 us
  local copies, waits for them, and re-layouts: 3.77 us -> 0.66 us
    pallas_call x1, Pallas kernels: 46.3 us -> 42.9 us  [body(): pl.pallas_call(kernel, out_shape=pltpu.VMEM(multipliers.shape, F32), in_s...]
    unnamed x2 -> x1, local copies, waits for them, and re-layouts: 3.77 us -> 0.66 us
where the time goes in v2:
time: 43.7 us; the launch traced here: 43.6 us
  Pallas kernels  42.9 us (98%)
  local copies, waits for them, and re-layouts  0.66 us (2%)
    pallas_call x1, Pallas kernels, body(): pl.pallas_call(kernel, out_shape=pltpu.VMEM(multipliers.shape, F32), in_s...  42.9 us

profile of v2, /device:TPU:1, one launch (start us, length us, event | category | flops | bytes accessed | tf_op | source)
XLA Modules:
  0.0 43.6 jit_solution(13806551137292499818)
XLA Ops:
  0.0 42.9 %shard_map.64 = f32[16,4,512]{2,1,0:T(4,128)S(1)} custom-call(f32[16,4,512]{2,1,0:T(4,128)} %mult_h.1, f32[6,4,512]{2,1,0:T(4,128)} %own_h.1, f32[6,4,512]{2,1,0:T(4,128)} %near_h.1, s32[4,512]{1,0:T(4,128)} %face_h.1, s32[6,2048]{1,0:T(8,128)} %bitcast.1, f32[192,1536]{1,0:T(8,128)} %coarse_h.1), custom_call_target="tpu_custom_call" | custom-call | tf_op jit(solution)/shard_map/pallas_call | solution.py:322
  42.9 0.7 %copy.8 = f32[16,4,512]{2,1,0:T(4,128)} copy(f32[16,4,512]{2,1,0:T(4,128)S(1)} %shard_map.64) | data formatting | bytes 262144
